TPU v7x, 32 devices: a whole 2x2x4 slice. The times are simulated.
32 devices in a mesh: bunch: 8 (over z, x), dom: 4 (over y, core).
Axes of the slice: x: 2, y: 2, z: 4, core: 2. Of those that a mesh axis runs over, the one named last changes fastest.
Arguments:
- positions: float32 [2, 2, 16, 4096], P(None, None, 'bunch', 'dom'), may hold values from 0 to 127
- momenta: float32 [2, 2, 16, 4096], P(None, None, 'bunch', 'dom'), may hold values from -6 to 6
- kernel_hat: float32 [2, 2, 256, 256], replicated, may hold values from -1.2 to 1.2
- partners: int32 [2, 16, 16], P(None, 'bunch'), may hold values from 0 to 15, as said below
- offsets: int32 [2, 2, 16, 16], P(None, None, 'bunch'), may hold values from -32 to 32
- counts: int32 [2, 16], P(None, 'bunch'), may hold values from 1 to 16, as said below
Outputs:
- kicked: float32 [2, 2, 16, 4096], P(None, None, 'bunch', 'dom')
Inputs may be any that keep to these rules, and one draw needn't show every extreme that they name: partners[e, b, s] // 2 lies at most 2 from b // 2, counted around a cycle of 8 blocks. `counts`: the first bunch of each block of 2 bunches has all 16 slots live.
All inputs are finite; a program needn't handle non-finite values.
Results may differ from a plain program's by a relative error of at most 0.0003.
Values sent between devices are 32-bit elements; how exact they have to be, the bound alone decides.
A program may use at most 64 MiB of HBM per device.

v0:
```python
import math

import jax
import jax.numpy as jnp
from jax import lax
from jax.sharding import PartitionSpec as P

HOPS = 2


HIGH = lax.Precision.HIGHEST


def passed_along(x, axis, by):
    peers = lax.axis_size(axis)
    return lax.ppermute(x, axis, [(i, (i + by) % peers) for i in range(peers)])


def hat_table(coord, cells):
    centres = jnp.arange(cells, dtype=jnp.float32)
    return jnp.maximum(0.0, 1.0 - jnp.abs(coord[:, None] - centres[None, :]))


def product(left, right):
    return jnp.dot(left, right, precision=HIGH, preferred_element_type=jnp.float32)


def deposit(coords, cells):
    weight_x = hat_table(coords[0], cells)
    weight_y = hat_table(coords[1], cells)
    return product(weight_x.T, weight_y)


def kick(coords, fields, moments, cells):
    weight_x = hat_table(coords[0], cells)
    weight_y = hat_table(coords[1], cells)
    field_x = jnp.sum(product(weight_x, fields[0]) * weight_y, axis=1)
    field_y = jnp.sum(product(weight_x, fields[1]) * weight_y, axis=1)
    return moments + jnp.stack([field_x, field_y])


def transform_fields(summed, kernel, cosine, sine, cells):
    padded_cells = cosine.shape[0]
    real_rows = product(cosine, summed)
    imag_rows = -product(sine, summed)
    spec_real = product(real_rows, cosine) + product(imag_rows, sine)
    spec_imag = product(imag_rows, cosine) - product(real_rows, sine)
    cos_rows = cosine[:cells]
    sin_rows = sine[:cells]
    cos_cols = cosine[:, :cells]
    sin_cols = sine[:, :cells]
    results = []
    for component in range(2):
        kernel_real = kernel[component, 0]
        kernel_imag = kernel[component, 1]
        prod_real = kernel_real * spec_real - kernel_imag * spec_imag
        prod_imag = kernel_real * spec_imag + kernel_imag * spec_real
        half_real = product(cos_rows, prod_real) - product(sin_rows, prod_imag)
        half_imag = product(cos_rows, prod_imag) + product(sin_rows, prod_real)
        result = product(half_real, cos_cols) - product(half_imag, sin_cols)
        results.append(result / float(padded_cells * padded_cells))
    return jnp.stack(results)


def window_of(grids):
    pieces = []
    for step in range(-HOPS, HOPS + 1):
        if step == 0:
            pieces.append(grids)
        else:
            pieces.append(passed_along(grids, "bunch", -step))
    return jnp.stack(pieces)


def per_device(positions, momenta, kernel_hat, partners, offsets, counts):
    bpb = positions.shape[2]
    local = 2 * bpb
    parts = positions.shape[3]
    padded_cells = kernel_hat.shape[-1]
    cells = padded_cells // 2
    slots = partners.shape[-1]
    device = lax.axis_index("bunch")
    ndev = lax.axis_size("bunch")
    coords = jnp.transpose(positions.reshape(2, local, parts), (1, 0, 2))
    partial_value = lax.map(lambda item: deposit(item, cells), coords)
    shares = lax.psum_scatter(partial_value, "dom", scatter_dimension=0, tiled=True)
    window_part = window_of(shares)
    window = lax.all_gather(window_part, "dom", axis=1, tiled=True)
    share_len = local // lax.axis_size("dom")
    targets = lax.axis_index("dom") * share_len + jnp.arange(share_len, dtype=jnp.int32)
    flat = window.reshape(-1, cells, cells)
    indices = jnp.arange(padded_cells, dtype=jnp.int32)
    angle = (indices[:, None] * indices[None, :] % padded_cells).astype(jnp.float32) * (
        2.0 * math.pi / padded_cells
    )
    cosine = jnp.cos(angle)
    sine = jnp.sin(angle)
    grid_cells = jnp.arange(cells, dtype=jnp.int32)
    slot_ids = jnp.arange(slots, dtype=jnp.int32)

    def field_of(target):
        beam = target // bpb
        member = target % bpb
        row = partners[beam, member]
        shift_x = offsets[0, beam, member]
        shift_y = offsets[1, beam, member]
        live_count = counts[beam, member]
        other = (1 - beam) * bpb
        relative = (row // bpb - device + HOPS) % ndev
        chosen_rows = relative * local + other + row % bpb
        chosen = jnp.take(flat, chosen_rows, axis=0)
        live = (slot_ids < live_count).astype(jnp.float32)
        target_x = (grid_cells[None, None, :] + shift_x[:, None, None]) % padded_cells
        target_y = (grid_cells[None, None, :] + shift_y[:, None, None]) % padded_cells
        place_x = (indices[None, :, None] == target_x).astype(jnp.float32) * live[:, None, None]
        place_y = (indices[None, :, None] == target_y).astype(jnp.float32)
        moved = jnp.einsum(
            "sri,sij->srj", place_x, chosen, precision=HIGH, preferred_element_type=jnp.float32
        )
        summed = jnp.einsum(
            "srj,sqj->rq", moved, place_y, precision=HIGH, preferred_element_type=jnp.float32
        )
        return transform_fields(summed, kernel_hat, cosine, sine, cells)

    fields = lax.map(field_of, targets)
    fields = lax.all_gather(fields, "dom", axis=0, tiled=True)
    moments = jnp.transpose(momenta.reshape(2, local, parts), (1, 0, 2))
    kicked = lax.map(lambda item: kick(item[0], item[1], item[2], cells), (coords, fields, moments))
    return jnp.transpose(kicked, (1, 0, 2)).reshape(2, 2, bpb, parts)


def solution(mesh):
    in_specs = (
        P(None, None, "bunch", "dom"),
        P(None, None, "bunch", "dom"),
        P(),
        P(None, "bunch", None),
        P(None, None, "bunch", None),
        P(None, "bunch"),
    )
    out_specs = P(None, None, "bunch", "dom")
    return jax.shard_map(
        per_device, mesh=mesh, in_specs=in_specs, out_specs=out_specs, check_vma=False
    )
```

profile of v0, /device:TPU:0, one launch (start us, length us, event | category | flops | bytes accessed | tf_op | source)
XLA Modules:
  0.0 106.3 jit_solution(3857685599385187216)
XLA Ops:
  7.4 7.8 %while.24 = (s32[]{:T(128)}, f32[4,128,128]{2,1,0:T(8,128)}, f32[4,2,1024]{2,1,0:T(2,128)S(1)}, s32[]{:T(128)}, s32[]{:T(128)}, /*index=5*/s32[]{}) while((s32[]{:T(128)}, f32[4,128,128]{2,1,0:T(8,128)}, f32[4,2,1024]{2,1,0:T(2,128)S(1)}, s32[]{:T(128)}, s32[]{:T(128)}, /*index=5*/s32[]{}) %tuple.55), condition=%wide.region_1.2_spmd, body=%wide.region_0.1_spmd.sunk | while | flops 202375168 | bytes 90713 | solution.py:85
  7.4 1.9 %fusion.158 = f32[4,128,128]{2,1,0:T(8,128)} fusion(f32[4,128,128]{2,1,0:T(8,128)} %get-tuple-element.186, s32[]{:T(128)} %get-tuple-element.185, f32[1024]{0:T(1024)S(1)} %bitcast.151, f32[1024]{0:T(1024)S(1)} %bitcast.150), kind=kOutput, calls=%fused_computation.2.clone.1 | convolution fusion | flops 202375168 | bytes 74240 | tf_op jit(solution)/shard_map/while/body/eval_jaxpr/dot_general | solution.py:25
  9.4 1.9 %fusion.158 = f32[4,128,128]{2,1,0:T(8,128)} fusion(f32[4,128,128]{2,1,0:T(8,128)} %get-tuple-element.186, s32[]{:T(128)} %get-tuple-element.185, f32[1024]{0:T(1024)S(1)} %bitcast.151, f32[1024]{0:T(1024)S(1)} %bitcast.150), kind=kOutput, calls=%fused_computation.2.clone.1 | convolution fusion | flops 202375168 | bytes 74240 | tf_op jit(solution)/shard_map/while/body/eval_jaxpr/dot_general | solution.py:25
  11.3 1.9 %fusion.158 = f32[4,128,128]{2,1,0:T(8,128)} fusion(f32[4,128,128]{2,1,0:T(8,128)} %get-tuple-element.186, s32[]{:T(128)} %get-tuple-element.185, f32[1024]{0:T(1024)S(1)} %bitcast.151, f32[1024]{0:T(1024)S(1)} %bitcast.150), kind=kOutput, calls=%fused_computation.2.clone.1 | convolution fusion | flops 202375168 | bytes 74240 | tf_op jit(solution)/shard_map/while/body/eval_jaxpr/dot_general | solution.py:25
  13.2 1.9 %fusion.158 = f32[4,128,128]{2,1,0:T(8,128)} fusion(f32[4,128,128]{2,1,0:T(8,128)} %get-tuple-element.186, s32[]{:T(128)} %get-tuple-element.185, f32[1024]{0:T(1024)S(1)} %bitcast.151, f32[1024]{0:T(1024)S(1)} %bitcast.150), kind=kOutput, calls=%fused_computation.2.clone.1 | convolution fusion | flops 202375168 | bytes 74240 | tf_op jit(solution)/shard_map/while/body/eval_jaxpr/dot_general | solution.py:25
  15.2 22.9 %reduce-scatter.2.cloned.1.call-done = f32[1,128,128]{2,1,0:T(8,128)} async-done(((f32[4,128,128]{2,1,0:T(8,128)}), f32[1,128,128]{2,1,0:T(8,128)}) %reduce-scatter.2.cloned.1.call-update) | async-done | bytes 65552 | tf_op jit(solution)/shard_map/reduce_scatter | solution.py:86
  38.1 1.5 %collective-permute-start = (f32[1,128,128]{2,1,0:T(8,128)}, f32[1,128,128]{2,1,0:T(8,128)S(1)}, u32[]{:S(2)}, u32[]{:S(2)}) collective-permute-start(f32[1,128,128]{2,1,0:T(8,128)} %reduce-scatter.2.cloned.1.call-done), channel_id=1, source_target_pairs={{0,8},{4,12},{8,16},{12,20},{16,24},{20,28},{24,0},{28,4},{1,9},{5... | collective-permute-start | bytes 196616 | tf_op jit(solution)/shard_map/ppermute | solution.py:16
  39.6 1.5 %collective-permute-start.1 = (f32[1,128,128]{2,1,0:T(8,128)}, f32[1,128,128]{2,1,0:T(8,128)S(1)}, u32[]{:S(2)}, u32[]{:S(2)}) collective-permute-start(f32[1,128,128]{2,1,0:T(8,128)} %reduce-scatter.2.cloned.1.call-done), channel_id=1, source_target_pairs={{0,4},{4,8},{8,12},{12,16},{16,20},{20,24},{24,28},{28,0},{1,5},{5... | collective-permute-start | bytes 196616 | tf_op jit(solution)/shard_map/ppermute | solution.py:16
  41.1 3.2 %collective-permute-start.2 = (f32[1,128,128]{2,1,0:T(8,128)}, f32[1,128,128]{2,1,0:T(8,128)S(1)}, u32[]{:S(2)}, u32[]{:S(2)}) collective-permute-start(f32[1,128,128]{2,1,0:T(8,128)} %reduce-scatter.2.cloned.1.call-done), channel_id=1, source_target_pairs={{0,28},{4,0},{8,4},{12,8},{16,12},{20,16},{24,20},{28,24},{1,29},{... | collective-permute-start | bytes 196616 | tf_op jit(solution)/shard_map/ppermute | solution.py:16
  44.9 2.5 %collective-permute-done.1 = f32[1,128,128]{2,1,0:T(8,128)S(1)} collective-permute-done((f32[1,128,128]{2,1,0:T(8,128)}, f32[1,128,128]{2,1,0:T(8,128)S(1)}, u32[]{:S(2)}, u32[]{:S(2)}) %collective-permute-start.1) | collective-permute-done | bytes 65568 | tf_op jit(solution)/shard_map/ppermute | solution.py:16
  51.8 1.0 fusion.58
  52.8 1.0 fusion.57
  53.9 12.5 %all-gather.3.cloned.1.call-done = f32[5,4,128,128]{3,2,1,0:T(8,128)} async-done(((f32[5,1,128,128]{3,2,1,0:T(8,128)}), f32[5,4,128,128]{3,2,1,0:T(8,128)}) %all-gather.3.cloned.1.call-update) | async-done | bytes 1310736 | tf_op jit(solution)/shard_map/all_gather | solution.py:88
  66.4 1.9 %gather_fusion = f32[16,128,128]{2,1,0:T(8,128)S(1)} fusion(f32[20,128,128]{2,1,0:T(8,128)} %bitcast.145, s32[1024]{0:T(1024)S(1)} %pad_clamp_fusion), kind=kCustom, calls=%fused_computation | custom fusion | bytes 2097216 | tf_op jit(solution)/shard_map/while/body/eval_jaxpr/jit(_take)/gather | solution.py:111
  68.3 2.3 %fusion.32 = f32[16,256,128]{2,1,0:T(8,128)S(1)} fusion(f32[16,128,128]{2,1,0:T(8,128)S(1)} %gather_fusion, f32[16]{0:T(128)S(1)} %get-tuple-element.120, s32[16,128]{1,0:T(8,128)S(1)} %add_select_fusion.2, pred[16]{0:T(512)(128)(4,1)S(1)} %get-tuple-element.119), kind=kOutput, calls=%fused_computation.46 | convolution fusion | flops 806617088 | bytes 3154000 | tf_op jit(solution)/shard_map/while/body/eval_jaxpr/sri,sij->srj/dot_general | solution.py:117
  70.6 1.4 %fusion.35 = f32[256,256]{1,0:T(8,128)S(1)} fusion(f32[16,256,128]{2,1,0:T(8,128)S(1)} %fusion.32, s32[16,128]{1,0:T(8,128)S(1)} %add_select_fusion.1), kind=kOutput, calls=%fused_computation.53 | convolution fusion | flops 1611137024 | bytes 2367488 | tf_op jit(solution)/shard_map/while/body/eval_jaxpr/srj,sqj->rq/dot_general | solution.py:120
  72.0 1.8 %convolution_negate_fusion = f32[256,256]{1,0:T(8,128)S(1)} fusion(f32[256,256]{1,0:T(8,128)S(1)} %fusion.35), kind=kOutput, calls=%fused_computation.52 | convolution fusion | flops 202309632 | bytes 524288 | tf_op jit(solution)/shard_map/while/body/eval_jaxpr/dot_general | solution.py:25
  73.8 1.6 %fusion.63 = f32[256,256]{1,0:T(8,128)S(1)} fusion(f32[256,256]{1,0:T(8,128)S(1)} %fusion.35), kind=kOutput, calls=%fused_computation.97 | convolution fusion | flops 202244096 | bytes 524288 | tf_op jit(solution)/shard_map/while/body/eval_jaxpr/dot_general | solution.py:25
  75.4 1.4 %fusion.59 = f32[256,256]{1,0:T(8,128)S(1)} fusion(f32[256,256]{1,0:T(8,128)S(1)} %convolution_negate_fusion), kind=kOutput, calls=%fused_computation.95 | convolution fusion | flops 202244096 | bytes 524288 | tf_op jit(solution)/shard_map/while/body/eval_jaxpr/dot_general | solution.py:25
  76.7 1.3 %fusion.61 = f32[256,256]{1,0:T(8,128)S(1)} fusion(f32[256,256]{1,0:T(8,128)S(1)} %fusion.63), kind=kOutput, calls=%fused_computation.96 | convolution fusion | flops 202244096 | bytes 524288 | tf_op jit(solution)/shard_map/while/body/eval_jaxpr/dot_general | solution.py:25
  78.1 1.4 %convolution_subtract_fusion = f32[256,256]{1,0:T(8,128)S(1)} fusion(f32[256,256]{1,0:T(8,128)S(1)} %fusion.59, f32[256,256]{1,0:T(8,128)S(1)} %fusion.63), kind=kOutput, calls=%fused_computation.50 | convolution fusion | flops 202309632 | bytes 786432 | tf_op jit(solution)/shard_map/while/body/eval_jaxpr/dot_general | solution.py:25
  79.5 2.6 %fusion.53 = (f32[256,256]{1,0:T(8,128)S(1)}, f32[256,256]{1,0:T(8,128)S(1)}, f32[256,256]{1,0:T(8,128)S(1)}, f32[256,256]{1,0:T(8,128)S(1)}) fusion(f32[256,256]{1,0:T(8,128)S(1)} %convolution_subtract_fusion, f32[2,2,256,256]{3,2,1,0:T(8,128)} %param.12, f32[256,256]{1,0:T(8,128)S(1)} %fusion.61, f32[256,256]{1,0:T(8,128)S(1)} %convolution_negate_fusion), kind=kOutput, calls=%fused_computation.86 | convolution fusion | flops 203096064 | bytes 2883584 | tf_op jit(solution)/shard_map/while/body/eval_jaxpr/dot_general | solution.py:25
  85.5 7.2 %all-gather = f32[8,128,128]{2,1,0:T(8,128)S(1)} all-gather(f32[2,128,128]{2,1,0:T(8,128)S(1)} %pad_maximum_fusion), channel_id=2, replica_groups=mesh['bunch'=8,'dom'=4] {'dom'}, dimensions={0}, use_global_device_ids=true | all-gather | bytes 655360 | tf_op jit(solution)/shard_map/all_gather | solution.py:126
  92.7 6.1 %while.25 = (s32[]{:T(128)}, f32[4,2,1024]{2,1,0:T(2,128)S(1)}, f32[4,2,1024]{2,1,0:T(2,128)S(1)}, f32[4,2,1024]{2,1,0:T(2,128)S(1)}, f32[4,2,128,128]{3,2,1,0:T(8,128)S(1)}, /*index=5*/s32[]{:T(128)}, s32[]{:T(128)}, s32[]{}) while((s32[]{:T(128)}, f32[4,2,1024]{2,1,0:T(2,128)S(1)}, f32[4,2,1024]{2,1,0:T(2,128)S(1)}, ...), condition=%wide.region_6.7_spmd, body=%wide.region_3.6_spmd.sunk | while | flops 405276672 | bytes 196729 | solution.py:128
  (66 shorter events, 15.9 us)
Async XLA Ops:
  6.5 31.6 %reduce-scatter.2.cloned.1.call-start = ((), (), s32[]{:S(2)}) async-start(), calls=%async_computation.1 | async-start | bytes 327680 | tf_op jit(solution)/shard_map/reduce_scatter | solution.py:86
  7.3 42.3 %copy-start.1 = (f32[2,2,2,1024]{3,2,1,0:T(2,128)S(1)}, f32[2,2,2,1024]{3,2,1,0:T(2,128)}, u32[]{:S(2)}) copy-start(f32[2,2,2,1024]{3,2,1,0:T(2,128)} %param.11) | copy-start | bytes 98308
  7.3 42.3 %copy-start.3 = (s32[2,2]{1,0:T(2,128)S(1)}, s32[2,2]{1,0:T(2,128)}, u32[]{:S(2)}) copy-start(s32[2,2]{1,0:T(2,128)} %param.15) | copy-start | bytes 52
  7.3 43.0 %copy-start.2 = (s32[2,2,16]{2,1,0:T(2,128)S(1)}, s32[2,2,16]{2,1,0:T(2,128)}, u32[]{:S(2)}) copy-start(s32[2,2,16]{2,1,0:T(2,128)} %param.13) | copy-start | bytes 772
  15.2 51.2 %all-gather.3.cloned.1.call-start = ((), (), s32[]{:S(2)}) async-start(), calls=%async_computation.2 | async-start | bytes 1638400 | tf_op jit(solution)/shard_map/all_gather | solution.py:88
  38.1 6.8 %collective-permute-start = (f32[1,128,128]{2,1,0:T(8,128)}, f32[1,128,128]{2,1,0:T(8,128)S(1)}, u32[]{:S(2)}, u32[]{:S(2)}) collective-permute-start(f32[1,128,128]{2,1,0:T(8,128)} %reduce-scatter.2.cloned.1.call-done), channel_id=1, source_target_pairs={{0,8},{4,12},{8,16},{12,20},{16,24},{20,28},{24,0},{28,4},{1,9},{5... | collective-permute-start | bytes 196616 | tf_op jit(solution)/shard_map/ppermute | solution.py:16
  39.6 7.8 %collective-permute-start.1 = (f32[1,128,128]{2,1,0:T(8,128)}, f32[1,128,128]{2,1,0:T(8,128)S(1)}, u32[]{:S(2)}, u32[]{:S(2)}) collective-permute-start(f32[1,128,128]{2,1,0:T(8,128)} %reduce-scatter.2.cloned.1.call-done), channel_id=1, source_target_pairs={{0,4},{4,8},{8,12},{12,16},{16,20},{20,24},{24,28},{28,0},{1,5},{5... | collective-permute-start | bytes 196616 | tf_op jit(solution)/shard_map/ppermute | solution.py:16
  41.1 7.1 %collective-permute-start.2 = (f32[1,128,128]{2,1,0:T(8,128)}, f32[1,128,128]{2,1,0:T(8,128)S(1)}, u32[]{:S(2)}, u32[]{:S(2)}) collective-permute-start(f32[1,128,128]{2,1,0:T(8,128)} %reduce-scatter.2.cloned.1.call-done), channel_id=1, source_target_pairs={{0,28},{4,0},{8,4},{12,8},{16,12},{20,16},{24,20},{28,24},{1,29},{... | collective-permute-start | bytes 196616 | tf_op jit(solution)/shard_map/ppermute | solution.py:16
  44.3 4.5 %collective-permute-start.3 = (f32[1,128,128]{2,1,0:T(8,128)}, f32[1,128,128]{2,1,0:T(8,128)S(1)}, u32[]{:S(2)}, u32[]{:S(2)}) collective-permute-start(f32[1,128,128]{2,1,0:T(8,128)} %reduce-scatter.2.cloned.1.call-done), channel_id=1, source_target_pairs={{0,24},{4,28},{8,0},{12,4},{16,8},{20,12},{24,16},{28,20},{1,25},{... | collective-permute-start | bytes 196616 | tf_op jit(solution)/shard_map/ppermute | solution.py:16
  48.8 0.7 copy-start
Sparse Core Ops, SparseCore 0:
  15.3 22.7 reduce-scatter.1
  49.7 16.6 all-gather.2
where the time goes:
time: 107 us; the launch traced here: 106 us
  waiting for transfers between devices  38.5 us (36%)
  matrix products  30.6 us (29%)
  between operations  13.7 us (13%)
  blocking collectives  7.16 us (7%)
  starting transfers between devices  6.79 us (6%)
  local copies, waits for them, and re-layouts  6.46 us (6%)
  other arithmetic  2.95 us (3%)
    dot_general x30, matrix products, product(): jnp.dot(left, right, precision=HIGH, preferred_element_type=jnp.float32)  27 us
    reduce_scatter x1, waiting for transfers between devices, per_device(): lax.psum_scatter(partial_value, 'dom', scatter_dimension=0, tiled=True)  22.9 us
    all_gather x1, waiting for transfers between devices, per_device(): window = lax.all_gather(window_part, 'dom', axis=1, tiled=True)  12.5 us
    all_gather x1, blocking collectives, per_device(): fields = lax.all_gather(fields, 'dom', axis=0, tiled=True)  7.16 us
    ppermute x4, starting transfers between devices, passed_along(): return lax.ppermute(x, axis, [(i, (i + by) % peers) for i in range(peers)])  6.75 us
    ppermute x4, waiting for transfers between devices, passed_along(): return lax.ppermute(x, axis, [(i, (i + by) % peers) for i in range(peers)])  3.06 us
    unnamed x14, local copies, waits for them, and re-layouts  2.41 us
    dot_general x1, matrix products, field_of(): jnp.einsum('sri,sij->srj', place_x, chosen, precision=HIGH, preferred_ele...  2.25 us
  transfers between devices with their start and end apart: 6, of which 4 were waited for; matrix products, arithmetic and copies ran while one was open for 5% of the time, Pallas kernels for 0%

commit v1 on v0

v1 whole, which is shorter than its diff:
```python
import functools

import jax
import jax.numpy as jnp
import ml_dtypes
import numpy as np
from jax import lax
from jax.experimental import pallas as pl
from jax.experimental.pallas import tpu as pltpu
from jax.sharding import PartitionSpec as P

HOPS = 2
OFFSET = 32
LANES = 256
MESH = pl.DeviceIdType.MESH
BF = jnp.bfloat16
F32 = jnp.float32


def split(x):
    high = x.astype(BF)
    return high, (x - high.astype(F32)).astype(BF)


def dot(a, b):
    return jnp.dot(a, b, preferred_element_type=F32)


def dot3(ah, al, bh, bl):
    return dot(ah, bh) + dot(ah, bl) + dot(al, bh)


def hat(row, cells):
    centres = lax.broadcasted_iota(jnp.int32, (cells, row.shape[1]), 0).astype(F32)
    return jnp.maximum(0.0, 1.0 - jnp.abs(row - centres))


def np_split(table):
    table = table.astype(np.float32)
    high = table.astype(ml_dtypes.bfloat16)
    low = (table - high.astype(np.float32)).astype(ml_dtypes.bfloat16)
    return np.stack([high, low])


def dft_tables(padded, cells, rows):
    k = np.arange(padded)

    def cs(left, right):
        angle = 2.0 * np.pi * (np.outer(left, right) % padded) / padded
        return np.cos(angle), np.sin(angle)

    c1, s1 = cs(k, np.arange(rows) - OFFSET)
    c2, s2 = cs(k, k)
    c3, s3 = cs(k, np.arange(cells))
    c4, s4 = cs(np.arange(cells), k)
    t1 = np.concatenate([c1, -s1], 0)
    t2 = np.concatenate([c2, s2], 0)
    t3 = np.block([[c3, s3], [-s3, c3]])
    t4 = np.concatenate([c4, -s4], 1) / float(padded * padded)
    return [np_split(t) for t in (t1, t2, t3, t4)]


def body(
    nb, nd, bpb, cells, padded, parts, slots,
    partners, offsets, counts, pos, mom, kernel_hbm, t1_hbm, t2_hbm, t3_hbm, t4_hbm,
    out,
    pos_s, rx, tx, ty, win, wx, wy, src, res, fin, kern, t1, t2, t3, t4,
    pos_send, pos_recv, win_send, win_recv, mate_send, mate_recv, res_send, res_recv, load_sem,
):
    local = 2 * bpb
    b = lax.axis_index("bunch")
    d = lax.axis_index("dom")
    beam = lax.div(d, bpb)
    member = lax.rem(d, bpb)
    source = lax.rem(d + bpb, local)
    pad = 2 * OFFSET
    rows = cells + pad

    def at(block, dom):
        return (block, dom)

    barrier = pltpu.get_barrier_semaphore()
    jumps = [j for h in range(1, HOPS + 1) for j in (h, -h)]
    for k in range(1, nd):
        pl.semaphore_signal(barrier, inc=1, device_id=at(b, lax.rem(d + k, nd)), device_id_type=MESH)
    for j in jumps:
        pl.semaphore_signal(barrier, inc=1, device_id=at(lax.rem(b + j + nb, nb), d), device_id_type=MESH)

    loads = [
        pltpu.make_async_copy(a, v, load_sem.at[i])
        for i, (a, v) in enumerate(
            [(t1_hbm, t1), (t2_hbm, t2), (kernel_hbm, kern), (t3_hbm, t3), (t4_hbm, t4)]
        )
    ]
    for load in loads:
        load.start()
    for e in range(2):
        for m in range(bpb):
            for c in range(2):
                pos_s[e * bpb + m, c : c + 1, :] = pos[c, e, m : m + 1, :]
    zero = jnp.zeros((2 * HOPS + 1, bpb, pad, cells), F32)
    win[:, :, :pad, :] = zero
    win[:, :, pad + cells :, :] = zero
    pl.semaphore_wait(barrier, nd - 1 + len(jumps))

    sends = []
    for which in range(2):
        for k in range(1, nd):
            peer = lax.rem(d + k, nd)
            bunch = lax.rem(peer + bpb, local) if which == 0 else peer
            copy = pltpu.make_async_remote_copy(
                src_ref=pos_s.at[bunch],
                dst_ref=rx.at[k - 1, which],
                send_sem=pos_send.at[k - 1, which],
                recv_sem=pos_recv.at[k - 1, which],
                device_id=at(b, peer),
                device_id_type=MESH,
            )
            copy.start()
            sends.append(copy)

    def fill(coords):
        for p in range(0, parts, LANES):
            sl = slice(p, p + LANES)
            high, low = split(hat(coords[0:1, sl], cells))
            tx[:cells, sl] = high
            tx[cells:, sl] = low
            high, low = split(hat(coords[1:2, sl], cells))
            ty[:cells, sl] = high
            ty[cells:, sl] = low
        return lax.dot_general(
            tx[...], ty[...], (((1,), (1,)), ((), ())), preferred_element_type=F32
        )

    total = fill(pos_s[source])
    for k in range(1, nd):
        sends[k - 1].wait_recv()
        total = total + fill(rx[k - 1, 0])
    grid = (
        total[:cells, :cells] + total[:cells, cells:] + total[cells:, :cells] + total[cells:, cells:]
    )
    band = pl.ds(pad, cells)
    win[HOPS, member, band, :] = grid

    grid_sends = {}
    for i, j in enumerate(jumps):
        copy = pltpu.make_async_remote_copy(
            src_ref=win.at[HOPS, member, band],
            dst_ref=win.at[HOPS - j, member, band],
            send_sem=win_send.at[i],
            recv_sem=win_recv.at[i],
            device_id=at(lax.rem(b + j + nb, nb), d),
            device_id_type=MESH,
        )
        copy.start()
        grid_sends[j] = copy
    mate_sends = []

    def to_mates(place):
        for k in range(1, bpb):
            mate = beam * bpb + lax.rem(member + k, bpb)
            copy = pltpu.make_async_remote_copy(
                src_ref=win.at[place, member, band],
                dst_ref=win.at[place, member, band],
                send_sem=mate_send.at[place, k - 1],
                recv_sem=mate_recv.at[place, k - 1],
                device_id=at(b, mate),
                device_id_type=MESH,
            )
            copy.start()
            mate_sends.append((place, k, copy))

    to_mates(HOPS)

    def kick_tables(coords, base):
        for p in range(0, parts, LANES):
            sl = slice(p, p + LANES)
            to = slice(base + p, base + p + LANES)
            wx[:, to] = hat(coords[0:1, sl], cells)
            high, low = split(hat(coords[1:2, sl], cells))
            wy[:cells, to] = high
            wy[cells : 2 * cells, to] = high
            wy[2 * cells :, to] = low

    kick_tables(pos_s[d], 0)
    for k in range(1, nd):
        sends[nd - 1 + k - 1].wait_recv()
        kick_tables(rx[k - 1, 1], k * parts)

    for j in jumps:
        grid_sends[j].wait_recv()
        to_mates(HOPS - j)
    for place, k, copy in mate_sends:
        copy.wait_recv()

    live_count = counts[beam, member]
    lane = lax.broadcasted_iota(jnp.int32, (8, cells), 1)
    chosen = []
    for s in range(slots):
        row = partners[beam, member, s]
        place = jnp.minimum(lax.rem(lax.div(row, bpb) - b + HOPS + nb, nb), 2 * HOPS)
        shift_x = offsets[0, beam, member, s]
        shift_y = offsets[1, beam, member, s]
        turn = jnp.where(shift_y < 0, shift_y + cells, shift_y)
        live = jnp.where(s < live_count, 1.0, 0.0).astype(F32)
        wrap = jnp.where(shift_y < 0, 1, 0)
        upper = jnp.where(lane >= turn, 1, 0)
        first = jnp.where(upper != wrap, live, 0.0)
        chosen.append((place, lax.rem(row, bpb), OFFSET - shift_x, turn, first, live - first))
    step = 2 * OFFSET
    for r in range(0, rows, step):
        low_half = jnp.zeros((step, cells), F32)
        high_half = jnp.zeros((step, cells), F32)
        for place, which, start, turn, first, second in chosen:
            piece = win[place, which, pl.ds(start + r, step), :]
            piece = pltpu.roll(piece, turn, 1)
            low_half = low_half + piece * jnp.concatenate([first] * (step // 8), 0)
            high_half = high_half + piece * jnp.concatenate([second] * (step // 8), 0)
        src[r : r + step, :cells] = low_half
        src[r : r + step, cells:] = high_half

    loads[0].wait()
    sh, sl = split(src[...])
    spec = dot3(t1[0], t1[1], sh, sl)
    real, imag = spec[:padded], spec[padded:]
    ah, al = split(real)
    bh, bl = split(imag)

    def pair(x, y):
        return jnp.concatenate(
            [jnp.concatenate([x, y], 1), jnp.concatenate([y, -x], 1)], 0
        )

    loads[1].wait()
    spec = dot3(pair(ah, bh), pair(al, bl), t2[0], t2[1])
    real, imag = spec[:padded], spec[padded:]
    loads[2].wait()
    mixed = []
    for c in range(2):
        kr, ki = kern[c, 0], kern[c, 1]
        mixed.append(jnp.concatenate([kr * real - ki * imag, kr * imag + ki * real], 1))
    mh, ml = split(jnp.concatenate(mixed, 0))
    loads[3].wait()
    half = dot3(mh, ml, t3[0], t3[1])
    g0, g1 = half[:padded], half[padded:]
    stacked = jnp.concatenate(
        [
            jnp.concatenate([g0[:, :cells], g1[:, :cells]], 1),
            jnp.concatenate([g0[:, cells:], g1[:, cells:]], 1),
        ],
        0,
    )
    gh, gl = split(stacked)
    loads[4].wait()
    field = dot3(t4[0], t4[1], gh, gl)
    fh, fl = split(jnp.concatenate([field[:, :cells], field[:, cells:]], 0))
    weights = jnp.concatenate([fh, fl, fh], 1)

    def kicks(k):
        for p in range(0, parts, LANES):
            sl = slice(k * parts + p, k * parts + p + LANES)
            z = dot(weights, wy[:, sl])
            w = wx[:, sl]
            for c in range(2):
                row = jnp.sum(z[c * cells : (c + 1) * cells] * w, axis=0, keepdims=True)
                res[k, c : c + 1, p : p + LANES] = row

    res_sends = []
    for k in range(1, nd):
        kicks(k)
        copy = pltpu.make_async_remote_copy(
            src_ref=res.at[k],
            dst_ref=fin.at[d],
            send_sem=res_send.at[k - 1],
            recv_sem=res_recv.at[k - 1],
            device_id=at(b, lax.rem(d - k + nd, nd)),
            device_id_type=MESH,
        )
        copy.start()
        res_sends.append(copy)
    kicks(0)
    fin[d] = res[0]
    for copy in res_sends:
        copy.wait_recv()
    for e in range(2):
        for m in range(bpb):
            for c in range(2):
                out[c, e, m : m + 1, :] = mom[c, e, m : m + 1, :] + fin[e * bpb + m, c : c + 1, :]
    for copy in sends + list(grid_sends.values()) + res_sends:
        copy.wait_send()
    for _, _, copy in mate_sends:
        copy.wait_send()


def solution(mesh):
    nb, nd = mesh.shape["bunch"], mesh.shape["dom"]

    def per_device(positions, momenta, kernel_hat, partners, offsets, counts):
        bpb = positions.shape[2]
        parts = positions.shape[3]
        padded = kernel_hat.shape[-1]
        cells = padded // 2
        slots = partners.shape[-1]
        local = 2 * bpb
        assert local == nd and nb > 2 * HOPS
        pad = 2 * OFFSET
        rows = cells + pad
        tables = [jnp.asarray(t) for t in dft_tables(padded, cells, rows)]
        vmem = pl.BlockSpec(memory_space=pltpu.VMEM)
        smem = pl.BlockSpec(memory_space=pltpu.SMEM)
        anym = pl.BlockSpec(memory_space=pl.ANY)
        dma = pltpu.SemaphoreType.DMA
        return pl.pallas_call(
            functools.partial(body, nb, nd, bpb, cells, padded, parts, slots),
            out_shape=jax.ShapeDtypeStruct(momenta.shape, F32),
            in_specs=[smem] * 3 + [vmem] * 2 + [anym] * 5,
            out_specs=vmem,
            scratch_shapes=[
                pltpu.VMEM((local, 2, parts), F32),
                pltpu.VMEM((nd - 1, 2, 2, parts), F32),
                pltpu.VMEM((2 * cells, parts), BF),
                pltpu.VMEM((2 * cells, parts), BF),
                pltpu.VMEM((2 * HOPS + 1, bpb, cells + 2 * pad, cells), F32),
                pltpu.VMEM((cells, nd * parts), F32),
                pltpu.VMEM((3 * cells, nd * parts), BF),
                pltpu.VMEM((rows, padded), F32),
                pltpu.VMEM((nd, 2, parts), F32),
                pltpu.VMEM((local, 2, parts), F32),
                pltpu.VMEM(kernel_hat.shape, F32),
            ]
            + [pltpu.VMEM(t.shape, BF) for t in tables]
            + [
                dma((nd - 1, 2)),
                dma((nd - 1, 2)),
                dma((2 * HOPS,)),
                dma((2 * HOPS,)),
                dma((2 * HOPS + 1, bpb - 1)),
                dma((2 * HOPS + 1, bpb - 1)),
                dma((nd - 1,)),
                dma((nd - 1,)),
                dma((5,)),
            ],
            compiler_params=pltpu.CompilerParams(collective_id=0, has_side_effects=True),
            name="beam_kick",
        )(partners, offsets, counts, positions, momenta, kernel_hat, *tables)

    spec = P(None, None, "bunch", "dom")
    return jax.shard_map(
        per_device,
        mesh=mesh,
        in_specs=(spec, spec, P(), P(None, "bunch", None), P(None, None, "bunch", None), P(None, "bunch")),
        out_specs=spec,
        check_vma=False,
    )
```

time: 107 us -> 25.9 us (0.24)
  waiting for transfers between devices: 38.5 us -> 0 us
  matrix products: 30.6 us -> 0 us
  Pallas kernels: 0 us -> 24.2 us
  between operations: 13.7 us -> 0.01 us
  blocking collectives: 7.16 us -> 0 us
  starting transfers between devices: 6.79 us -> 0 us
  local copies, waits for them, and re-layouts: 6.46 us -> 1.38 us
  other arithmetic: 2.95 us -> 0 us
    dot_general x32 -> x0, matrix products: 30.6 us -> none  [the longest x30 27 us: product(): jnp.dot(left, right, precision=HIGH, preferred_element_type=jnp.float32)]
    pallas_call x0 -> x1, Pallas kernels: none -> 24.2 us  [per_device(): pl.pallas_call(functools.partial(body, nb, nd, bpb, cells, padded, parts,...]
    reduce_scatter x1 -> x0, waiting for transfers between devices: 22.9 us -> none  [per_device(): lax.psum_scatter(partial_value, 'dom', scatter_dimension=0, tiled=True)]
    all_gather x1 -> x0, waiting for transfers between devices: 12.5 us -> none  [per_device(): window = lax.all_gather(window_part, 'dom', axis=1, tiled=True)]
    all_gather x1 -> x0, blocking collectives: 7.16 us -> none  [per_device(): fields = lax.all_gather(fields, 'dom', axis=0, tiled=True)]
    ppermute x4 -> x0, starting transfers between devices: 6.75 us -> none  [passed_along(): return lax.ppermute(x, axis, [(i, (i + by) % peers) for i in range(peers)])]
    ppermute x4 -> x0, waiting for transfers between devices: 3.06 us -> none  [passed_along(): return lax.ppermute(x, axis, [(i, (i + by) % peers) for i in range(peers)])]
    gather x1 -> x0, local copies, waits for them, and re-layouts: 1.93 us -> none  [field_of(): chosen = jnp.take(flat, chosen_rows, axis=0)]
  transfers between devices with their start and end apart: 6 -> 0, of which waited for: 4 -> 0; matrix products, arithmetic and copies ran while one was open for 5% -> 0% of each run, Pallas kernels for 0% -> 0%
where the time goes in v1:
time: 25.9 us; the launch traced here: 25.6 us
  Pallas kernels  24.2 us (93%)
  local copies, waits for them, and re-layouts  1.38 us (5%)
    pallas_call x1, Pallas kernels, per_device(): pl.pallas_call(functools.partial(body, nb, nd, bpb, cells, padded, parts,...  24.2 us
    unnamed x1, local copies, waits for them, and re-layouts  1.38 us

profile of v1, /device:TPU:0, one launch (start us, length us, event | category | flops | bytes accessed | tf_op | source)
XLA Modules:
  0.0 25.6 jit_solution(554828639881402479)
XLA Ops:
  0.0 24.2 %beam_kick.1 = f32[2,2,2,1024]{3,2,1,0:T(2,128)} custom-call(s32[2,2,16]{2,1,0:T(2,128)} %partners.1, s32[2,2,2,16]{3,2,1,0:T(2,128)} %offsets.1, s32[2,2]{1,0:T(2,128)} %counts.1, f32[2,2,2,1024]{3,2,1,0:T(2,128)} %pos.1, f32[2,2,2,1024]{3,2,1,0:T(2,128)} %mom.1, f32[2,2,256,256]{3,2,1,0:T(8,128)} %kernel_hbm.1, bf16[2,512,192]{2,1,0:T(8,128)(2,1)} %constant.8.clone.t1_hbm, ...), custom_call_target="tpu_custom_call" | custom-call | tf_op jit(solution)/shard_map/beam_kick/pallas_call | solution.py:313
  24.3 1.4 %copy.12 = f32[2,2,2,1024]{3,2,1,0:T(2,128)} copy(f32[2,2,2,1024]{3,2,1,0:T(2,128)} %beam_kick.1) | data formatting | bytes 65536

commit v2 on v1

--- a/solution.py
+++ b/solution.py
@@ -33,6 +33,18 @@
 def hat(row, cells):
     centres = lax.broadcasted_iota(jnp.int32, (cells, row.shape[1]), 0).astype(F32)
     return jnp.maximum(0.0, 1.0 - jnp.abs(row - centres))
+
+
+def hat_split(row, cells):
+    below = jnp.floor(row)
+    above = below + 1.0
+    h0, l0 = split(1.0 - jnp.abs(row - below))
+    h1, l1 = split(1.0 - jnp.abs(row - above))
+    centres = lax.broadcasted_iota(jnp.int32, (cells, row.shape[1]), 0).astype(F32).astype(BF)
+    at0 = centres == below.astype(BF)
+    at1 = centres == above.astype(BF)
+    none = jnp.zeros((), BF)
+    return jnp.where(at0, h0, jnp.where(at1, h1, none)), jnp.where(at0, l0, jnp.where(at1, l1, none))
 
 
 def np_split(table):
@@ -62,7 +74,7 @@
 
 def body(
     nb, nd, bpb, cells, padded, parts, slots,
-    partners, offsets, counts, pos, mom, kernel_hbm, t1_hbm, t2_hbm, t3_hbm, t4_hbm,
+    partners, offsets, counts, pos, kernel_hbm, t1_hbm, t2_hbm, t3_hbm, t4_hbm,
     out,
     pos_s, rx, tx, ty, win, wx, wy, src, res, fin, kern, t1, t2, t3, t4,
     pos_send, pos_recv, win_send, win_recv, mate_send, mate_recv, res_send, res_recv, load_sem,
@@ -101,6 +113,31 @@
     zero = jnp.zeros((2 * HOPS + 1, bpb, pad, cells), F32)
     win[:, :, :pad, :] = zero
     win[:, :, pad + cells :, :] = zero
+    def fill(coords):
+        for p in range(0, parts, LANES):
+            sl = slice(p, p + LANES)
+            high, low = hat_split(coords[0:1, sl], cells)
+            tx[:cells, sl] = high
+            tx[cells:, sl] = low
+            high, low = hat_split(coords[1:2, sl], cells)
+            ty[:cells, sl] = high
+            ty[cells:, sl] = low
+        return lax.dot_general(
+            tx[...], ty[...], (((1,), (1,)), ((), ())), preferred_element_type=F32
+        )
+
+    def kick_tables(coords, base):
+        for p in range(0, parts, LANES):
+            sl = slice(p, p + LANES)
+            to = slice(base + p, base + p + LANES)
+            wx[:, to] = hat(coords[0:1, sl], cells)
+            high, low = hat_split(coords[1:2, sl], cells)
+            wy[:cells, to] = high
+            wy[cells : 2 * cells, to] = high
+            wy[2 * cells :, to] = low
+
+    total = fill(pos_s[source])
+    kick_tables(pos_s[d], 0)
     pl.semaphore_wait(barrier, nd - 1 + len(jumps))
 
     sends = []
@@ -119,20 +156,6 @@
             copy.start()
             sends.append(copy)
 
-    def fill(coords):
-        for p in range(0, parts, LANES):
-            sl = slice(p, p + LANES)
-            high, low = split(hat(coords[0:1, sl], cells))
-            tx[:cells, sl] = high
-            tx[cells:, sl] = low
-            high, low = split(hat(coords[1:2, sl], cells))
-            ty[:cells, sl] = high
-            ty[cells:, sl] = low
-        return lax.dot_general(
-            tx[...], ty[...], (((1,), (1,)), ((), ())), preferred_element_type=F32
-        )
-
-    total = fill(pos_s[source])
     for k in range(1, nd):
         sends[k - 1].wait_recv()
         total = total + fill(rx[k - 1, 0])
@@ -172,21 +195,9 @@
 
     to_mates(HOPS)
 
-    def kick_tables(coords, base):
-        for p in range(0, parts, LANES):
-            sl = slice(p, p + LANES)
-            to = slice(base + p, base + p + LANES)
-            wx[:, to] = hat(coords[0:1, sl], cells)
-            high, low = split(hat(coords[1:2, sl], cells))
-            wy[:cells, to] = high
-            wy[cells : 2 * cells, to] = high
-            wy[2 * cells :, to] = low
-
-    kick_tables(pos_s[d], 0)
     for k in range(1, nd):
         sends[nd - 1 + k - 1].wait_recv()
         kick_tables(rx[k - 1, 1], k * parts)
-
     for j in jumps:
         grid_sends[j].wait_recv()
         to_mates(HOPS - j)
@@ -285,7 +296,7 @@
     for e in range(2):
         for m in range(bpb):
             for c in range(2):
-                out[c, e, m : m + 1, :] = mom[c, e, m : m + 1, :] + fin[e * bpb + m, c : c + 1, :]
+                out[c, e, m : m + 1, :] = fin[e * bpb + m, c : c + 1, :]
     for copy in sends + list(grid_sends.values()) + res_sends:
         copy.wait_send()
     for _, _, copy in mate_sends:
@@ -310,10 +321,10 @@
         smem = pl.BlockSpec(memory_space=pltpu.SMEM)
         anym = pl.BlockSpec(memory_space=pl.ANY)
         dma = pltpu.SemaphoreType.DMA
-        return pl.pallas_call(
+        kicks = pl.pallas_call(
             functools.partial(body, nb, nd, bpb, cells, padded, parts, slots),
             out_shape=jax.ShapeDtypeStruct(momenta.shape, F32),
-            in_specs=[smem] * 3 + [vmem] * 2 + [anym] * 5,
+            in_specs=[smem] * 3 + [vmem] + [anym] * 5,
             out_specs=vmem,
             scratch_shapes=[
                 pltpu.VMEM((local, 2, parts), F32),
@@ -342,7 +353,8 @@
             ],
             compiler_params=pltpu.CompilerParams(collective_id=0, has_side_effects=True),
             name="beam_kick",
-        )(partners, offsets, counts, positions, momenta, kernel_hat, *tables)
+        )(partners, offsets, counts, positions, kernel_hat, *tables)
+        return momenta + kicks
 
     spec = P(None, None, "bunch", "dom")
     return jax.shard_map(

time: 25.9 us -> 26.1 us (level)
  other arithmetic: 0 us -> 1.39 us
  local copies, waits for them, and re-layouts: 1.38 us -> 0.01 us
    add x0 -> x1, other arithmetic: none -> 1.39 us  [per_device(): return momenta + kicks]
    unnamed x1 -> x2, local copies, waits for them, and re-layouts: 1.38 us -> 0.01 us
where the time goes in v2:
time: 26.1 us; the launch traced here: 25.8 us
  Pallas kernels  24.4 us (93%)
  other arithmetic  1.39 us (5%)
    pallas_call x1, Pallas kernels, per_device(): pl.pallas_call(functools.partial(body, nb, nd, bpb, cells, padded, parts,...  24.4 us
    add x1, other arithmetic, per_device(): return momenta + kicks  1.39 us

profile of v2, /device:TPU:0, one launch (start us, length us, event | category | flops | bytes accessed | tf_op | source)
XLA Modules:
  0.0 25.8 jit_solution(4136452800738186295)
XLA Ops:
  0.0 0.0 copy-start
  0.0 24.4 %beam_kick.1 = f32[2,2,2,1024]{3,2,1,0:T(2,128)} custom-call(s32[2,2,16]{2,1,0:T(2,128)} %partners.1, s32[2,2,2,16]{3,2,1,0:T(2,128)} %offsets.1, s32[2,2]{1,0:T(2,128)} %counts.1, f32[2,2,2,1024]{3,2,1,0:T(2,128)} %pos.1, f32[2,2,256,256]{3,2,1,0:T(8,128)} %kernel_hbm.1, bf16[2,512,192]{2,1,0:T(8,128)(2,1)} %constant.8.clone.t1_hbm, ...), custom_call_target="tpu_custom_call" | custom-call | tf_op jit(solution)/shard_map/beam_kick/pallas_call | solution.py:324
  24.4 0.0 copy-done
  24.4 1.4 %add.3 = f32[2,2,2,1024]{3,2,1,0:T(2,128)} add(f32[2,2,2,1024]{3,2,1,0:T(2,128)S(1)} %copy-done, f32[2,2,2,1024]{3,2,1,0:T(2,128)} %beam_kick.1) | non-fusion elementwise | flops 8192 | bytes 98304 | tf_op jit(solution)/shard_map/add | solution.py:357
Async XLA Ops:
  0.0 24.4 %copy-start = (f32[2,2,2,1024]{3,2,1,0:T(2,128)S(1)}, f32[2,2,2,1024]{3,2,1,0:T(2,128)}, u32[]{:S(2)}) copy-start(f32[2,2,2,1024]{3,2,1,0:T(2,128)} %param.11) | copy-start | bytes 98308
